TPU v7x, 32 devices: a whole 2x2x4 slice. The times are simulated.
32 devices in a mesh: dp: 16 (over z, y, x), mp: 2 (over core).
Axes of the slice: x: 2, y: 2, z: 4, core: 2. Of those that a mesh axis runs over, the one named last changes fastest.
Arguments:
- attn: bfloat16 [6144, 1536], P('dp', 'mp'), may hold values from -6 to 6
- w_out: bfloat16 [1536, 1536], P('mp'), may hold values from -0.15625 to 0.15625
- resid: bfloat16 [6144, 1536], P('dp', 'mp'), may hold values from -6 to 6
- target: bfloat16 [6144, 1536], P('dp', 'mp'), may hold values from -6 to 6
- gate: float32 [48, 1536], P('dp', 'mp'), may hold values from -5 to 5
- bins: int32 [48], P('dp'), may hold values from 0 to 127
Outputs:
- grad_w_out: float32 [1536, 1536], P('dp', 'mp')
- grad_gate: float32 [48, 1536], P('dp', 'mp')
- bin_loss: float32 [128], replicated
All inputs are finite; a program needn't handle non-finite values.
Results may differ from a plain program's by a relative error of at most 0.0008.
Values may be sent and summed in bfloat16 or wider, within the bound.
A program may use at most 64 MiB of HBM per device.

v0:
```python
import math
import jax
import jax.numpy as jnp
from jax import lax
from jax.sharding import PartitionSpec as P

NBINS = 128
LOSS_SCALE = 4096.0


def bin_weights():
    centre = (jnp.arange(NBINS).astype(jnp.float32) + 0.5) / NBINS
    logit = jnp.log(centre) - jnp.log(1.0 - centre)
    return jnp.exp(-0.5 * logit * logit) / (math.sqrt(2.0 * math.pi) * centre * (1.0 - centre))


def shards(attn, w_out, resid, target, gate, bins):
    samples = bins.shape[0]
    tok_rows = attn.shape[0]
    per_sample = tok_rows // samples
    full_width = w_out.shape[1]
    own_cols = resid.shape[1]
    bin_ids = jnp.arange(NBINS, dtype=jnp.int32)
    one_hot = (bins[:, None] == bin_ids[None, :]).astype(jnp.float32)
    local_counts = jnp.sum(one_hot, axis=0)
    weights = bin_weights()
    counts = lax.psum(local_counts, "dp")
    whole_attn = lax.all_gather(attn, "mp", axis=1, tiled=True)
    partial_value = jnp.dot(attn, w_out, preferred_element_type=jnp.float32)
    projected = lax.psum_scatter(partial_value, "mp", scatter_dimension=1, tiled=True)
    proj_cube = projected.reshape(samples, per_sample, own_cols)
    hidden = (
        resid.reshape(samples, per_sample, own_cols).astype(jnp.float32)
        + gate[:, None, :] * proj_cube
    )
    error_cube = hidden - target.reshape(samples, per_sample, own_cols).astype(jnp.float32)
    sample_error = jnp.sum(error_cube * error_cube, axis=(1, 2)) / (per_sample * full_width)
    bin_part = jnp.sum(one_hot * sample_error[:, None], axis=0)
    sums = lax.psum(bin_part, ("dp", "mp"))
    floored = jnp.maximum(counts, 1.0)
    scale_bin = LOSS_SCALE * weights / floored
    coefficient = jnp.sum(one_hot * scale_bin[None, :], axis=1) * (2.0 / (per_sample * full_width))
    d_hidden = coefficient[:, None, None] * error_cube
    grad_gate = jnp.sum(d_hidden * proj_cube, axis=1)
    d_proj = (d_hidden * gate[:, None, :]).astype(jnp.bfloat16).reshape(tok_rows, own_cols)
    full_grad = lax.dot_general(
        whole_attn, d_proj, (((0,), (0,)), ((), ())), preferred_element_type=jnp.float32
    )
    grad_out = lax.psum_scatter(full_grad, "dp", scatter_dimension=0, tiled=True)
    bin_loss = weights * sums / floored
    return (grad_out, grad_gate, bin_loss)


def solution(mesh):
    return jax.shard_map(
        shards,
        mesh=mesh,
        in_specs=(
            P("dp", "mp"),
            P("mp", None),
            P("dp", "mp"),
            P("dp", "mp"),
            P("dp", "mp"),
            P("dp"),
        ),
        out_specs=(P("dp", "mp"), P("dp", "mp"), P()),
        check_vma=False,
    )
```

profile of v0, /device:TPU:0, one launch (start us, length us, event | category | flops | bytes accessed | tf_op | source)
XLA Modules:
  0.0 214.0 jit_solution(4137970757654208983)
XLA Ops:
  7.2 0.0 copy-start
  7.2 0.0 reduce-scatter.5.cloned.1.call-start
  7.2 1.6 copy-done
  8.8 3.6 %fusion.5 = f32[384,1536]{1,0:T(8,128)} fusion(bf16[384,768]{1,0:T(8,128)(2,1)} %param.6, bf16[768,1536]{1,0:T(8,128)(2,1)S(1)} %copy-done), kind=kOutput, calls=%fused_computation.21 | convolution fusion | flops 905969664 | bytes 5308416 | tf_op jit(solution)/shard_map/dot_general | solution.py:29
  12.4 0.0 reduce-scatter.5.cloned.1.call-update
  12.4 0.0 all-gather.2.cloned.1.call-start
  12.5 0.7 all-gather.2.cloned.1.call-update
  13.2 0.0 reduce-scatter.7.cloned.1.call-start
  13.2 0.0 copy-done.5
  13.2 0.1 convert_reduce_fusion
  13.3 43.5 %psum.14 = f32[128]{0:T(128)S(1)} all-reduce(f32[128]{0:T(128)S(1)} %convert_reduce_fusion), channel_id=1, replica_groups=mesh['dp'=16,'mp'=2] {'dp'}, use_global_device_ids=true, to_apply=%region_1.0 | all-reduce | flops 128 | bytes 1024 | tf_op jit(solution)/shard_map/psum | solution.py:27
  56.8 0.5 multiply_divide_fusion.1
  57.4 0.0 copy-done.7
  57.4 0.0 copy-done.4
  57.4 0.0 copy-start.1
  57.4 0.0 copy-start.2
  57.4 0.0 copy-start.3
  57.4 2.1 multiply_reduce_fusion
  59.5 0.1 bitcast_reduce_fusion
  59.6 0.0 copy-done.6
  59.6 0.6 select_reduce_fusion
  60.2 0.1 broadcast_bitcast_fusion
  60.3 0.0 copy-done.1
  60.3 0.0 copy-done.2
  60.3 1.1 fusion.2
  61.4 5.0 %convolution_bitcast_fusion = f32[1536,768]{0,1:T(8,128)} fusion(bf16[384,768]{1,0:T(8,128)(2,1)} %fusion.2, bf16[384,1536]{1,0:T(8,128)(2,1)} %all-gather.2.cloned.1.call-done), kind=kOutput, calls=%fused_computation | convolution fusion | flops 905969664 | bytes 6488064 | tf_op jit(solution)/shard_map/dot_general | solution.py:46
  66.4 6.1 %copy.12 = f32[1536,768]{1,0:T(8,128)} copy(f32[1536,768]{0,1:T(8,128)} %convolution_bitcast_fusion) | data formatting | bytes 9437184
  72.6 0.0 reduce-scatter.7.cloned.1.call-update
  72.6 37.9 %psum.15 = f32[128]{0:T(128)} all-reduce(f32[128]{0:T(128)} %get-tuple-element.12), channel_id=1, replica_groups=mesh['dp'=16,'mp'=2] {'dp','mp'}, use_global_device_ids=true, to_apply=%region_9.10 | all-reduce | flops 128 | bytes 1024 | tf_op jit(solution)/shard_map/psum | solution.py:39
  110.5 1.2 multiply_divide_fusion
  111.7 2.2 %multiply_reduce_fusion.1 = f32[3,768]{1,0:T(4,128)} fusion(f32[3,128,768]{2,1,0:T(8,128)S(1)} %bitcast.29, f32[3]{0:T(128)S(1)} %broadcast_multiply_fusion.1, f32[3,768]{1,0:T(4,128)S(1)} %copy-done.4, bf16[3,128,768]{2,1,0:T(8,128)(2,1)} %bitcast.31, bf16[3,128,768]{2,1,0:T(8,128)(2,1)} %bitcast.30), kind=kLoop, calls=%fused_computation.7 | loop fusion | flops 2356992 | bytes 2377740 | tf_op jit(solution)/shard_map/reduce_sum | solution.py:44
  113.9 93.5 %reduce-scatter.7.cloned.1.call-done = f32[96,768]{1,0:T(8,128)} async-done(((f32[1536,768]{1,0:T(8,128)}), f32[96,768]{1,0:T(8,128)}) %reduce-scatter.7.cloned.1.call-update) | async-done | bytes 294928
  (9 shorter events, 0.0 us)
Async XLA Ops:
  7.2 1.7 copy-start
  7.2 50.2 %reduce-scatter.5.cloned.1.call-start = ((), (), s32[]{:S(2)}) async-start(), calls=%async_computation.2 | async-start | bytes 3538944 | tf_op jit(solution)/shard_map/reduce_scatter | solution.py:30
  12.4 0.8 copy-start.5
  12.4 45.0 %copy-start.4 = (f32[3,768]{1,0:T(4,128)S(1)}, f32[3,768]{1,0:T(4,128)}, u32[]{:S(2)}) copy-start(f32[3,768]{1,0:T(4,128)} %param.10) | copy-start | bytes 27652
  12.4 49.0 %all-gather.2.cloned.1.call-start = ((), (), s32[]{:S(2)}) async-start(), calls=%async_computation.3 | async-start | bytes 1769472 | tf_op jit(solution)/shard_map/all_gather | solution.py:28
  13.2 194.3 %reduce-scatter.7.cloned.1.call-start = ((), (), s32[]{:S(2)}) async-start(), calls=%async_computation.4 | async-start | bytes 5013504
  56.8 0.5 copy-start.7
  57.4 2.3 %copy-start.6 = (f32[128]{0:T(128)S(1)}, f32[128]{0:T(128)}, u32[]{:S(2)}) copy-start(f32[128]{0:T(128)} %multiply_divide_fusion.1) | copy-start | bytes 1540
  57.4 2.9 %copy-start.1 = (f32[384,768]{1,0:T(8,128)S(1)}, f32[384,768]{1,0:T(8,128)}, u32[]{:S(2)}) copy-start(f32[384,768]{1,0:T(8,128)} %reduce-scatter.5.cloned.1.call-done) | copy-start | bytes 3538948
  57.4 2.9 %copy-start.2 = (bf16[384,768]{1,0:T(8,128)(2,1)S(1)}, bf16[384,768]{1,0:T(8,128)(2,1)}, u32[]{:S(2)}) copy-start(bf16[384,768]{1,0:T(8,128)(2,1)} %param.9) | copy-start | bytes 1769476
  57.4 2.9 %copy-start.3 = (bf16[384,768]{1,0:T(8,128)(2,1)S(1)}, bf16[384,768]{1,0:T(8,128)(2,1)}, u32[]{:S(2)}) copy-start(bf16[384,768]{1,0:T(8,128)(2,1)} %param.8) | copy-start | bytes 1769476
Sparse Core Ops, SparseCore 0:
  12.5 12.7 reduce-scatter.4
  26.8 10.5 all-gather.1
  72.7 134.7 reduce-scatter.6
where the time goes:
time: 214 us
  waiting for transfers between devices  94.3 us (44%)
  blocking collectives  81.4 us (38%)
  between operations  13.8 us (6%)
  matrix products  8.55 us (4%)
  other arithmetic  7.99 us (4%)
  local copies, waits for them, and re-layouts  7.85 us (4%)
    unnamed x4, waiting for transfers between devices  94.3 us
    psum x1, blocking collectives, shards(): counts = lax.psum(local_counts, 'dp')  43.5 us
    psum x1, blocking collectives, shards(): sums = lax.psum(bin_part, ('dp', 'mp'))  37.9 us
    unnamed x17, local copies, waits for them, and re-layouts  7.78 us
    dot_general x1, matrix products, shards(): lax.dot_general(whole_attn, d_proj, (((0,), (0,)), ((), ())), preferred_e...  4.99 us
  transfers between devices with their start and end apart: 3, of which 1 were waited for; matrix products, arithmetic and copies ran while one was open for 4% of the time, Pallas kernels for 0%

commit v1 on v0

--- a/solution.py
+++ b/solution.py
@@ -36,7 +36,8 @@
     error_cube = hidden - target.reshape(samples, per_sample, own_cols).astype(jnp.float32)
     sample_error = jnp.sum(error_cube * error_cube, axis=(1, 2)) / (per_sample * full_width)
     bin_part = jnp.sum(one_hot * sample_error[:, None], axis=0)
-    sums = lax.psum(bin_part, ("dp", "mp"))
+    parts = lax.all_gather(bin_part, ("dp", "mp"), axis=0, tiled=False)
+    sums = parts.sum(axis=0)
     floored = jnp.maximum(counts, 1.0)
     scale_bin = LOSS_SCALE * weights / floored
     coefficient = jnp.sum(one_hot * scale_bin[None, :], axis=1) * (2.0 / (per_sample * full_width))

time: 214 us -> 215 us (level)
    psum x1 -> x0, blocking collectives: 37.9 us -> none  [shards(): sums = lax.psum(bin_part, ('dp', 'mp'))]
    all_gather x0 -> x1, blocking collectives: none -> 37.7 us  [shards(): parts = lax.all_gather(bin_part, ('dp', 'mp'), axis=0, tiled=False)]
    unnamed x17 -> x21, local copies, waits for them, and re-layouts: 7.78 us -> 8.25 us
where the time goes in v1:
time: 215 us; the launch traced here: 214 us
  waiting for transfers between devices  94 us (44%)
  blocking collectives  81.2 us (38%)
  between operations  13.8 us (6%)
  matrix products  8.59 us (4%)
  local copies, waits for them, and re-layouts  8.32 us (4%)
  other arithmetic  8.31 us (4%)
    unnamed x4, waiting for transfers between devices  94 us
    psum x1, blocking collectives, shards(): counts = lax.psum(local_counts, 'dp')  43.5 us
    all_gather x1, blocking collectives, shards(): parts = lax.all_gather(bin_part, ('dp', 'mp'), axis=0, tiled=False)  37.7 us
    unnamed x21, local copies, waits for them, and re-layouts  8.25 us
    dot_general x1, matrix products, shards(): lax.dot_general(whole_attn, d_proj, (((0,), (0,)), ((), ())), preferred_e...  5.04 us
  transfers between devices with their start and end apart: 3, of which 1 were waited for; matrix products, arithmetic and copies ran while one was open for 4% of the time, Pallas kernels for 0%

profile of v1, /device:TPU:0, one launch (start us, length us, event | category | flops | bytes accessed | tf_op | source)
XLA Modules:
  0.0 214.3 jit_solution(12898686166609804845)
XLA Ops:
  7.2 0.0 copy-start
  7.2 0.0 reduce-scatter.5.cloned.1.call-start
  7.2 1.6 copy-done
  8.8 3.6 %fusion.5 = f32[384,1536]{1,0:T(8,128)} fusion(bf16[384,768]{1,0:T(8,128)(2,1)} %param.6, bf16[768,1536]{1,0:T(8,128)(2,1)S(1)} %copy-done), kind=kOutput, calls=%fused_computation.21 | convolution fusion | flops 905969664 | bytes 5308416 | tf_op jit(solution)/shard_map/dot_general | solution.py:29
  12.4 0.0 reduce-scatter.5.cloned.1.call-update
  12.4 0.0 all-gather.4.cloned.1.call-start
  12.5 0.7 all-gather.4.cloned.1.call-update
  13.2 0.0 reduce-scatter.7.cloned.1.call-start
  13.2 0.0 copy-done.6
  13.2 0.1 convert_reduce_fusion
  13.3 43.5 %psum.7 = f32[128]{0:T(128)S(1)} all-reduce(f32[128]{0:T(128)S(1)} %convert_reduce_fusion), channel_id=1, replica_groups=mesh['dp'=16,'mp'=2] {'dp'}, use_global_device_ids=true, to_apply=%region_1.0 | all-reduce | flops 128 | bytes 1024 | tf_op jit(solution)/shard_map/psum | solution.py:27
  56.8 0.5 multiply_divide_fusion.1
  57.4 0.0 copy-done.9
  57.4 0.0 copy-done.4
  57.4 0.0 copy-start.8
  57.4 0.0 copy-start.1
  57.4 0.0 copy-start.2
  57.4 0.0 copy-start.3
  57.4 2.1 multiply_reduce_fusion
  59.5 0.1 bitcast_reduce_fusion
  59.6 0.2 select_reduce_fusion
  59.8 0.6 copy-done.5
  60.4 0.1 broadcast_bitcast_fusion
  60.5 1.1 fusion.2
  61.6 5.0 %convolution_bitcast_fusion = f32[1536,768]{0,1:T(8,128)} fusion(bf16[384,768]{1,0:T(8,128)(2,1)} %fusion.2, bf16[384,1536]{1,0:T(8,128)(2,1)} %all-gather.4.cloned.1.call-done), kind=kOutput, calls=%fused_computation | convolution fusion | flops 905969664 | bytes 6488064 | tf_op jit(solution)/shard_map/dot_general | solution.py:47
  66.6 6.0 %copy.12 = f32[1536,768]{1,0:T(8,128)} copy(f32[1536,768]{0,1:T(8,128)} %convolution_bitcast_fusion) | data formatting | bytes 9437184
  72.7 0.0 reduce-scatter.7.cloned.1.call-update
  72.7 37.7 %all-gather.1 = f32[32,1,128]{2,1,0:T(1,128)} all-gather(f32[1,1,128]{2,1,0:T(1,128)S(1)} %bitcast.33), channel_id=2, replica_groups=mesh['dp'=16,'mp'=2] {'dp','mp'}, dimensions={0}, use_global_device_ids=true | all-gather | bytes 16896 | tf_op jit(solution)/shard_map/all_gather | solution.py:39
  110.4 0.8 reduce_sum.68
  111.1 1.2 multiply_divide_fusion
  112.3 2.2 %multiply_reduce_fusion.1 = f32[3,768]{1,0:T(4,128)} fusion(f32[3,128,768]{2,1,0:T(8,128)S(1)} %bitcast.30, f32[3]{0:T(128)} %copy-done.5, f32[3,768]{1,0:T(4,128)S(1)} %copy-done.4, bf16[3,128,768]{2,1,0:T(8,128)(2,1)} %bitcast.32, bf16[3,128,768]{2,1,0:T(8,128)(2,1)} %bitcast.31), kind=kLoop, calls=%fused_computation.7 | loop fusion | flops 2356992 | bytes 2377740 | tf_op jit(solution)/shard_map/reduce_sum | solution.py:45
  114.5 93.3 %reduce-scatter.7.cloned.1.call-done = f32[96,768]{1,0:T(8,128)} async-done(((f32[1536,768]{1,0:T(8,128)}), f32[96,768]{1,0:T(8,128)}) %reduce-scatter.7.cloned.1.call-update) | async-done | bytes 294928
  (14 shorter events, 0.0 us)
Async XLA Ops:
  7.2 1.7 copy-start
  7.2 50.2 %reduce-scatter.5.cloned.1.call-start = ((), (), s32[]{:S(2)}) async-start(), calls=%async_computation.2 | async-start | bytes 3538944 | tf_op jit(solution)/shard_map/reduce_scatter | solution.py:30
  12.4 0.8 copy-start.6
  12.4 45.0 %copy-start.4 = (f32[3,768]{1,0:T(4,128)S(1)}, f32[3,768]{1,0:T(4,128)}, u32[]{:S(2)}) copy-start(f32[3,768]{1,0:T(4,128)} %param.10) | copy-start | bytes 27652
  12.4 49.2 %all-gather.4.cloned.1.call-start = ((), (), s32[]{:S(2)}) async-start(), calls=%async_computation.3 | async-start | bytes 1769472 | tf_op jit(solution)/shard_map/all_gather | solution.py:28
  13.2 194.6 %reduce-scatter.7.cloned.1.call-start = ((), (), s32[]{:S(2)}) async-start(), calls=%async_computation.4 | async-start | bytes 5013504
  56.8 0.5 copy-start.9
  57.4 2.3 %copy-start.7 = (s32[3]{0:T(128)S(1)}, s32[3]{0:T(128)}, u32[]{:S(2)}) copy-start(s32[3]{0:T(128)} %param.11) | copy-start | bytes 40
  57.4 2.3 %copy-start.8 = (f32[128]{0:T(128)S(1)}, f32[128]{0:T(128)}, u32[]{:S(2)}) copy-start(f32[128]{0:T(128)} %multiply_divide_fusion.1) | copy-start | bytes 1540
  57.4 3.1 %copy-start.1 = (f32[384,768]{1,0:T(8,128)S(1)}, f32[384,768]{1,0:T(8,128)}, u32[]{:S(2)}) copy-start(f32[384,768]{1,0:T(8,128)} %reduce-scatter.5.cloned.1.call-done) | copy-start | bytes 3538948
  57.4 3.1 %copy-start.2 = (bf16[384,768]{1,0:T(8,128)(2,1)S(1)}, bf16[384,768]{1,0:T(8,128)(2,1)}, u32[]{:S(2)}) copy-start(bf16[384,768]{1,0:T(8,128)(2,1)} %param.9) | copy-start | bytes 1769476
  57.4 3.1 %copy-start.3 = (bf16[384,768]{1,0:T(8,128)(2,1)S(1)}, bf16[384,768]{1,0:T(8,128)(2,1)}, u32[]{:S(2)}) copy-start(bf16[384,768]{1,0:T(8,128)(2,1)} %param.8) | copy-start | bytes 1769476
  59.8 0.6 copy-start.5
Sparse Core Ops, SparseCore 0:
  12.5 12.7 reduce-scatter.4
  26.8 10.5 all-gather.3
  72.8 134.9 reduce-scatter.6
